TPU v7x, 32 devices: a whole 2x2x4 slice. The times are simulated.
32 devices in a mesh: row: 8 (over y, x, core), col: 4 (over z).
Axes of the slice: x: 2, y: 2, z: 4, core: 2. Of those that a mesh axis runs over, the one named last changes fastest.
Arguments:
- expression: bfloat16 [4096, 1024], P(('row', 'col')), may hold values from -200 to 200, as said below
- powers: int32 [10], replicated, may hold values from 1 to 20
Outputs:
- log_degree: float32 [10, 4096], P(None, ('row', 'col'))
- degree_freq: float32 [10, 10], replicated
- fit_slope: float32 [10], replicated
- mean_log: float32 [10], replicated
Inputs may be any that keep to these rules, and one draw needn't show every extreme that they name: Finite expression values.
All inputs are finite; a program needn't handle non-finite values.
Results may differ from a plain program's by a relative error of at most 0.0003.
Values may be sent and summed in bfloat16 or wider, within the bound.
A program may use at most 64 MiB of HBM per device.

v0:
```python
import jax
import jax.numpy as jnp
from jax import lax
from jax.sharding import PartitionSpec as P

BINS = 10


def gene_stats(genes):
    values = genes.astype(jnp.float32)
    gene_mean = jnp.mean(values, axis=1)
    centred = values - gene_mean[:, None]
    gene_inv = lax.rsqrt(jnp.mean(centred * centred, axis=1) + 1e-06)
    return (gene_mean, gene_inv)


def add_slice(totals, addend, start):
    current = lax.dynamic_slice_in_dim(totals, start, addend.shape[1], 1)
    return lax.dynamic_update_slice_in_dim(totals, current + addend, start, 1)


def block_sums(left_genes, right_genes, exponents, row_list, carry, left_start):
    row_count = left_genes.shape[0]
    block_rows = 256
    samples = left_genes.shape[1]
    left_mean, left_inv = gene_stats(left_genes)
    right_mean, right_inv = gene_stats(right_genes)

    def one_block(block_index, totals):
        row_totals, column_totals = totals
        offset = block_index * block_rows
        row_block = lax.dynamic_slice_in_dim(left_genes, offset, block_rows, 0)
        block_mean = lax.dynamic_slice_in_dim(left_mean, offset, block_rows, 0)
        block_inv = lax.dynamic_slice_in_dim(left_inv, offset, block_rows, 0)
        raw = lax.dot_general(
            row_block, right_genes, (((1,), (1,)), ((), ())), preferred_element_type=jnp.float32
        )
        pearson = (
            (raw / samples - block_mean[:, None] * right_mean[None, :])
            * block_inv[:, None]
            * right_inv[None, :]
        )
        log_abs = jnp.log(jnp.abs(pearson))
        row_parts = []
        for power_index in row_list:
            row_parts.append(jnp.sum(jnp.exp(exponents[power_index] * log_abs), axis=1))
        if row_parts:
            row_totals = add_slice(row_totals, jnp.stack(row_parts), left_start + offset)
        return (row_totals, column_totals)

    return lax.fori_loop(0, row_count // block_rows, one_block, carry)


def on_device(expression, powers):
    exponents = powers.astype(jnp.float32)
    npower = powers.shape[0]
    local_genes = expression.shape[0]
    row_width = local_genes * lax.axis_size("col")
    column_width = local_genes * lax.axis_size("row")
    row_list = list(range(npower))
    col_list = []
    initial = (
        jnp.zeros((len(row_list), row_width), jnp.float32),
        jnp.zeros((max(len(col_list), 1), column_width), jnp.float32),
    )
    left_genes = lax.all_gather(expression, "col", axis=0, tiled=True)
    row_totals, column_totals = block_sums(
        left_genes,
        lax.all_gather(expression, "row", axis=0, tiled=True),
        exponents,
        row_list,
        initial,
        0,
    )
    degree = lax.psum_scatter(row_totals, "col", scatter_dimension=1, tiled=True)
    peak = lax.pmax(jnp.max(degree, axis=1), ("row", "col"))
    position = jnp.clip(BINS * degree / peak[:, None] - 0.5, 0.0, BINS - 1.0)
    centres = jnp.arange(BINS, dtype=jnp.float32)
    weights = jnp.maximum(0.0, 1.0 - jnp.abs(position[:, :, None] - centres[None, None, :]))
    freq_total, degree_total = lax.psum(
        (jnp.sum(weights, axis=1), jnp.sum(degree, axis=1)), ("row", "col")
    )
    genes_all = local_genes * lax.axis_size("row") * lax.axis_size("col")
    degree_freq = freq_total / genes_all
    mean_log = jnp.log10(degree_total / genes_all)
    xfit = jnp.log10((centres[None, :] + 0.5) * peak[:, None] / BINS)
    yfit = jnp.log10(degree_freq + 1.0 / genes_all)
    xdev = xfit - jnp.mean(xfit, axis=1, keepdims=True)
    ydev = yfit - jnp.mean(yfit, axis=1, keepdims=True)
    fit_slope = jnp.sum(xdev * ydev, axis=1) / jnp.sum(xdev * xdev, axis=1)
    return (jnp.log10(degree), degree_freq, fit_slope, mean_log)


def solution(mesh):
    return jax.shard_map(
        on_device,
        mesh=mesh,
        in_specs=(P(("row", "col"), None), P()),
        out_specs=(P(None, ("row", "col")), P(), P(), P()),
        check_vma=False,
    )
```

profile of v0, /device:TPU:0, one launch (start us, length us, event | category | flops | bytes accessed | tf_op | source)
XLA Modules:
  0.0 201.4 jit_solution(1471055572352535315)
XLA Ops:
  7.2 0.7 all-gather.3.cloned.1.call-update
  7.9 0.7 all-gather.5.cloned.1.call-update
  8.7 0.7 convert_element_type.9
  9.4 30.9 %all-gather.3.cloned.1.call-done = bf16[512,1024]{1,0:T(8,128)(2,1)} async-done(((bf16[128,1024]{1,0:T(8,128)(2,1)}), bf16[512,1024]{1,0:T(8,128)(2,1)}) %all-gather.3.cloned.1.call-update) | async-done | bytes 1048592 | tf_op jit(solution)/shard_map/all_gather | solution.py:66
  40.3 1.4 convert_reduce_fusion.1
  41.7 1.6 fusion.10
  43.4 26.0 %all-gather.5.cloned.1.call-done = bf16[1024,1024]{1,0:T(8,128)(2,1)} async-done(((bf16[128,1024]{1,0:T(8,128)(2,1)}), bf16[1024,1024]{1,0:T(8,128)(2,1)}) %all-gather.5.cloned.1.call-update) | async-done | bytes 2097168 | tf_op jit(solution)/shard_map/all_gather | solution.py:69
  69.4 2.1 %convert_reduce_fusion = f32[1024]{0:T(1024)S(1)} fusion(bf16[1024,1024]{1,0:T(8,128)(2,1)} %all-gather.5.cloned.1.call-done), kind=kLoop, calls=%fused_computation.20 | loop fusion | flops 2096128 | bytes 2101248 | tf_op jit(solution)/shard_map/reduce_sum | solution.py:11
  71.5 0.1 copy-done
  71.6 0.7 fusion.8
  72.3 19.4 %while.13 = (s32[]{:T(128)}, f32[10,512]{1,0:T(8,128)S(1)}, f32[10]{0:T(128)S(1)}, bf16[512,1024]{1,0:T(8,128)(2,1)S(1)}, bf16[1024,1024]{1,0:T(8,128)(2,1)S(1)}...) while((s32[]{:T(128)}, f32[10,512]{1,0:T(8,128)S(1)}, ...), condition=%wide.region_15.0_spmd, body=%wide.region_4.0_spmd.sunk | while | flops 543686656 | bytes 2715955 | solution.py:51
  72.3 0.1 dynamic_slice.39
  72.4 0.1 dynamic_slice.40
  72.5 0.7 fusion.20
  73.2 8.8 %exponential_reduce_fusion.11 = (f32[256]{0:T(256)S(1)}, f32[256]{0:T(256)S(1)}, f32[256]{0:T(256)S(1)}, f32[256]{0:T(256)S(1)}, f32[256]{0:T(256)S(1)}, /*index...) fusion(f32[]{:T(128)} %bitcast.43, f32[]{:T(128)} %bitcast.44, ...), kind=kOutput, calls=%fused_computation.6.clone.1 | convolution fusion | flops 543684096 | bytes 2641964 | tf_op jit(solution)/shard_map/while/body/eval_jaxpr/dot_general | solution.py:35
  81.9 0.1 stack.78
  82.0 0.1 dynamic_slice.39
  82.1 0.1 dynamic_slice.40
  82.2 0.7 fusion.20
  82.9 8.8 %exponential_reduce_fusion.11 = (f32[256]{0:T(256)S(1)}, f32[256]{0:T(256)S(1)}, f32[256]{0:T(256)S(1)}, f32[256]{0:T(256)S(1)}, f32[256]{0:T(256)S(1)}, /*index...) fusion(f32[]{:T(128)} %bitcast.43, f32[]{:T(128)} %bitcast.44, ...), kind=kOutput, calls=%fused_computation.6.clone.1 | convolution fusion | flops 543684096 | bytes 2641964 | tf_op jit(solution)/shard_map/while/body/eval_jaxpr/dot_general | solution.py:35
  91.7 0.6 copy-done.2
  92.4 19.3 %reduce-scatter.2.cloned.1.call-done = f32[10,128]{1,0:T(8,128)} async-done(((f32[10,512]{1,0:T(8,128)}), f32[10,128]{1,0:T(8,128)}) %reduce-scatter.2.cloned.1.call-update) | async-done | bytes 5136 | tf_op jit(solution)/shard_map/reduce_scatter | solution.py:75
  111.7 0.8 fusion.14
  112.5 38.4 %pmax.7 = f32[10]{0:T(128)S(1)} all-reduce(f32[10]{0:T(128)S(1)} %get-tuple-element.170), channel_id=1, replica_groups=mesh['row'=8,'col'=4] {'row','col'}, use_global_device_ids=true, to_apply=%region_18.0 | all-reduce | flops 10 | bytes 80 | tf_op jit(solution)/shard_map/pmax | solution.py:76
  150.9 1.3 add_clamp_fusion
  152.2 0.1 maximum_reduce_fusion
  152.3 40.9 %all-reduce = (f32[10,10]{1,0:T(8,128)S(1)}, f32[10]{0:T(128)S(1)}) all-reduce(f32[10,10]{1,0:T(8,128)S(1)} %maximum_reduce_fusion, f32[10]{0:T(128)S(1)} %get-tuple-element.169), channel_id=1, replica_groups=mesh['row'=8,'col'=4] {'row','col'}, use_global_device_ids=true, to_apply=%region_20.21 | all-reduce | flops 110 | bytes 880 | tf_op jit(solution)/shard_map/psum | solution.py:80
  193.3 0.1 fusion.13
  193.4 0.2 fusion.12
  193.6 0.5 log_multiply_fusion.3
  194.1 0.2 multiply_reduce_fusion
  194.3 0.5 div.61
  (21 shorter events, 0.3 us)
Async XLA Ops:
  7.2 33.1 %all-gather.3.cloned.1.call-start = ((), (), s32[]{:S(2)}) async-start(), calls=%async_computation.1 | async-start | bytes 1310720 | tf_op jit(solution)/shard_map/all_gather | solution.py:66
  7.9 61.5 %all-gather.5.cloned.1.call-start = ((), (), s32[]{:S(2)}) async-start(), calls=%async_computation.2 | async-start | bytes 2359296 | tf_op jit(solution)/shard_map/all_gather | solution.py:69
  8.6 103.0 %reduce-scatter.2.cloned.1.call-start = ((), (), s32[]{:S(2)}) async-start(), calls=%async_computation.3 | async-start | bytes 40960 | tf_op jit(solution)/shard_map/reduce_scatter | solution.py:75
  69.4 2.2 %copy-start = (bf16[1024,1024]{1,0:T(8,128)(2,1)S(1)}, bf16[1024,1024]{1,0:T(8,128)(2,1)}, u32[]{:S(2)}) copy-start(bf16[1024,1024]{1,0:T(8,128)(2,1)} %all-gather.5.cloned.1.call-done) | copy-start | bytes 6291460
  69.4 2.9 %copy-start.1 = (bf16[512,1024]{1,0:T(8,128)(2,1)S(1)}, bf16[512,1024]{1,0:T(8,128)(2,1)}, u32[]{:S(2)}) copy-start(bf16[512,1024]{1,0:T(8,128)(2,1)} %all-gather.3.cloned.1.call-done) | copy-start | bytes 3145732
  91.7 0.6 copy-start.2
  193.4 1.5 copy-start.3
Sparse Core Ops, SparseCore 0:
  9.5 30.6 all-gather.2
  42.2 27.1 all-gather.4
  92.5 19.1 reduce-scatter.1
where the time goes:
time: 202 us; the launch traced here: 201 us
  blocking collectives  79.4 us (39%)
  waiting for transfers between devices  77.6 us (38%)
  matrix products  17.6 us (9%)
  between operations  13.8 us (7%)
  other arithmetic  10.3 us (5%)
  local copies, waits for them, and re-layouts  2.49 us (1%)
    psum x1, blocking collectives, on_device(): lax.psum((jnp.sum(weights, axis=1), jnp.sum(degree, axis=1)), ('row', 'co...  40.9 us
    pmax x1, blocking collectives, on_device(): peak = lax.pmax(jnp.max(degree, axis=1), ('row', 'col'))  38.4 us
    all_gather x1, waiting for transfers between devices, on_device(): left_genes = lax.all_gather(expression, 'col', axis=0, tiled=True)  30.9 us
    all_gather x1, waiting for transfers between devices, on_device(): lax.all_gather(expression, 'row', axis=0, tiled=True)  26 us
    reduce_scatter x1, waiting for transfers between devices, on_device(): lax.psum_scatter(row_totals, 'col', scatter_dimension=1, tiled=True)  19.3 us
    dot_general x2, matrix products, one_block(): lax.dot_general(row_block, right_genes, (((1,), (1,)), ((), ())), preferr...  17.6 us
  transfers between devices with their start and end apart: 3, of which 3 were waited for; matrix products, arithmetic and copies ran while one was open for 2% of the time, Pallas kernels for 0%

commit v1 on v0

v1 whole, which is shorter than its diff:
```python
import functools
import math

import jax
import jax.numpy as jnp
from jax import lax
from jax.experimental import pallas as pl
from jax.experimental.pallas import tpu as pltpu
from jax.sharding import PartitionSpec as P

BINS = 10
HALVES = 2
LOG2E = math.log2(math.e)
LOG10E = math.log10(math.e)
MESH = pl.DeviceIdType.MESH


def xor(value, mask):
    result, bit = value, 1
    while bit <= mask:
        if mask & bit:
            result = result + bit - 2 * bit * ((value // bit) % 2)
        bit *= 2
    return result


def gene_stats(block):
    values = block.astype(jnp.float32)
    mean = jnp.mean(values, axis=1, keepdims=True)
    centred = values - mean
    inv = lax.rsqrt(jnp.mean(centred * centred, axis=1, keepdims=True) + 1e-06)
    return mean, inv


def kernel(
    nr, nc, npower, powers_ref, expr_ref, log_degree_ref, freq_ref, slope_ref, mean_log_ref,
    left, right, right_mean, right_inv, partial, degrees,
    up_send, down_send, line_recv, plane_send, relay_send, plane_recv, part_send, part_recv, deg_send, deg_recv,
):
    r, c = lax.axis_index("row"), lax.axis_index("col")
    nq = nr // 2
    chip, core = r // 2, r % 2
    twin = r + 1 - 2 * core
    genes, samples = expr_ref.shape
    padded = partial.shape[2]
    rows = genes // HALVES
    genes_all = genes * nr * nc

    def chip_partner(k):
        return (xor(chip, k) if nq & (nq - 1) == 0 else (chip + k) % nq) * 2 + core

    def chip_source(k):
        return (xor(chip, k) if nq & (nq - 1) == 0 else (chip + nq - k) % nq) * 2 + core

    barrier = pltpu.get_barrier_semaphore()

    def greet_col(d, _):
        pl.semaphore_signal(barrier, inc=1, device_id=(r, (c + d) % nc), device_id_type=MESH)
        return 0

    def greet_row(d, _):
        pl.semaphore_signal(barrier, inc=1, device_id=((r + d) % nr, c), device_id_type=MESH)
        return 0

    lax.fori_loop(1, nc, greet_col, 0)
    lax.fori_loop(1, nr, greet_row, 0)

    left[c] = expr_ref[...]
    right[r] = expr_ref[...]
    exponents = [powers_ref[p].astype(jnp.float32) * LOG2E for p in range(npower)]

    def right_stats(index):
        mean, inv = gene_stats(right[index])
        right_mean[index] = jnp.broadcast_to(mean, (genes, 128))
        right_inv[index] = jnp.broadcast_to(inv, (genes, 128))

    right_stats(r)
    pl.semaphore_wait(barrier, nc - 1 + nr - 1)

    def line_copy(step, half, up):
        block = (c - step) if up else (c + step)
        window = pl.ds(half * rows, rows)
        block = jnp.clip(block, 0, nc - 1)
        target = jnp.clip(c + 1 if up else c - 1, 0, nc - 1)
        source = expr_ref.at[window] if step == 0 else left.at[block, window]
        return pltpu.make_async_remote_copy(
            src_ref=source,
            dst_ref=left.at[block, window],
            send_sem=(up_send if up else down_send).at[step, half],
            recv_sem=line_recv.at[block, half],
            device_id=(r, target),
            device_id_type=MESH,
        )

    def line_sends(step, up):
        return jnp.logical_and(c - step >= 0, c + 1 < nc) if up else jnp.logical_and(c + step < nc, c >= 1)

    def plane_copy(k):
        return pltpu.make_async_remote_copy(
            src_ref=expr_ref, dst_ref=right.at[r],
            send_sem=plane_send.at[k], recv_sem=plane_recv.at[r],
            device_id=(chip_partner(k), c), device_id_type=MESH,
        )

    def relay_copy(k):
        source = chip_source(k) if k else r
        return pltpu.make_async_remote_copy(
            src_ref=right.at[source] if k else expr_ref, dst_ref=right.at[source],
            send_sem=relay_send.at[k], recv_sem=plane_recv.at[source],
            device_id=(twin, c), device_id_type=MESH,
        )

    def plane_arrival(source):
        return pltpu.make_async_remote_copy(
            src_ref=expr_ref, dst_ref=right.at[source],
            send_sem=plane_send.at[0], recv_sem=plane_recv.at[source],
            device_id=(twin, c), device_id_type=MESH,
        )

    def line_arrival(step, half, up):
        block = jnp.clip((c - step) if up else (c + step), 0, nc - 1)
        window = pl.ds(half * rows, rows)
        return pltpu.make_async_remote_copy(
            src_ref=expr_ref.at[window], dst_ref=left.at[block, window],
            send_sem=up_send.at[0, half], recv_sem=line_recv.at[block, half],
            device_id=(r, c), device_id_type=MESH,
        )

    for half in range(HALVES):
        for up in (True, False):
            @pl.when(line_sends(0, up))
            def _():
                line_copy(0, half, up).start()
    for k in range(1, nq):
        plane_copy(k).start()
    relay_copy(0).start()

    def part_copy(d, block):
        return pltpu.make_async_remote_copy(
            src_ref=partial.at[c, block], dst_ref=partial.at[c, block],
            send_sem=part_send.at[d, block], recv_sem=part_recv.at[c, block],
            device_id=(r, (c + d) % nc), device_id_type=MESH,
        )

    def run_pass(block):
        genes_left = left[block]
        mean, inv = gene_stats(genes_left)
        mean_row = jnp.broadcast_to(mean, (genes, 128)).T[0:1, :]
        inv_row = jnp.broadcast_to(inv, (genes, 128)).T[0:1, :]

        def one_right(index, sums):
            raw = lax.dot_general(
                right[index], genes_left, (((1,), (1,)), ((), ())), preferred_element_type=jnp.float32
            )
            pearson = (raw * (1.0 / samples) - right_mean[index] * mean_row) * right_inv[index] * inv_row
            log_abs = jnp.log(jnp.abs(pearson))
            return tuple(
                sums[p] + jnp.sum(jnp.exp2(exponents[p] * log_abs).reshape(genes // 8, 8, genes), axis=0)
                for p in range(npower)
            )

        sums = lax.fori_loop(
            0, nr, one_right, tuple(jnp.zeros((8, genes), jnp.float32) for _ in range(npower)), unroll=2
        )
        lines = [jnp.sum(total, axis=0, keepdims=True) for total in sums]
        lines.append(jnp.zeros((padded - npower, genes), jnp.float32))
        partial[c, block] = jnp.concatenate(lines, axis=0)

        def send(d, _):
            part_copy(d, block).start()
            return 0

        lax.fori_loop(1, nc, send, 0)

    def line_step(step, half):
        for up in (True, False):
            @pl.when(c - step >= 0 if up else c + step < nc)
            def _():
                line_arrival(step, half, up).wait_recv()

            if step < nc - 1:
                @pl.when(line_sends(step, up))
                def _():
                    line_copy(step, half, up).start()

    def plane_step(k):
        if k:
            source = chip_source(k)
            plane_arrival(source).wait_recv()
            relay_copy(k).start()
            right_stats(source)

    def twin_step(k):
        source = chip_source(k) + 1 - 2 * core
        plane_arrival(source).wait_recv()
        right_stats(source)

    def passes(step):
        for up in (True, False):
            @pl.when(c - step >= 0 if up else c + step < nc)
            def _():
                run_pass(jnp.clip(c - step if up else c + step, 0, nc - 1))

    twin_step(0)
    todo = list(range(1, nq))
    for step in range(1, nc):
        last_plane = step == 2 or nc == 2
        for half in range(HALVES):
            line_step(step, half)
        if step == 1:
            for k in todo[: max(1, nq - 2)]:
                plane_step(k)
            for k in todo[: max(1, nq - 2)]:
                twin_step(k)
        if last_plane:
            for k in todo[max(1, nq - 2):]:
                plane_step(k)
            for k in todo[max(1, nq - 2):]:
                twin_step(k)
            run_pass(c)
            passes(1)
        if step >= 2:
            passes(step)

    def part_wait(d, _):
        source = (c + d) % nc

        def one(block, _):
            pltpu.make_async_remote_copy(
                src_ref=partial.at[c, block], dst_ref=partial.at[source, block],
                send_sem=part_send.at[d, block], recv_sem=part_recv.at[source, block],
                device_id=(r, source), device_id_type=MESH,
            ).wait_recv()
            return 0

        return lax.fori_loop(0, nc, one, 0)

    lax.fori_loop(1, nc, part_wait, 0)
    for block in range(nc):
        total = partial[0, block]
        for source in range(1, nc):
            total = total + partial[source, block]
        degrees[r, block] = total

    def deg_copy(d):
        return pltpu.make_async_remote_copy(
            src_ref=degrees.at[r], dst_ref=degrees.at[r],
            send_sem=deg_send.at[d], recv_sem=deg_recv.at[r],
            device_id=((r + d) % nr, c), device_id_type=MESH,
        )

    def deg_start(d, _):
        deg_copy(d).start()
        return 0

    def deg_wait(d, _):
        source = (r + d) % nr
        pltpu.make_async_remote_copy(
            src_ref=degrees.at[r], dst_ref=degrees.at[source],
            send_sem=deg_send.at[d], recv_sem=deg_recv.at[source],
            device_id=(source, c), device_id_type=MESH,
        ).wait_recv()
        return 0

    lax.fori_loop(1, nr, deg_start, 0)
    log_degree_ref[...] = (jnp.log(degrees[r, c]) * LOG10E)[:npower]

    for half in range(HALVES):
        for up in (True, False):
            for step in range(nc - 1):
                @pl.when(line_sends(step, up))
                def _():
                    line_copy(step, half, up).wait_send()
    for k in range(1, nq):
        plane_copy(k).wait_send()
    for k in range(nq):
        relay_copy(k).wait_send()

    def part_done(d, _):
        def one(block, _):
            part_copy(d, block).wait_send()
            return 0

        return lax.fori_loop(0, nc, one, 0)

    lax.fori_loop(1, nc, part_done, 0)
    lax.fori_loop(1, nr, deg_wait, 0)

    def peak_of(index, best):
        for block in range(nc):
            best = jnp.maximum(best, degrees[index, block])
        return best

    best = lax.fori_loop(0, nr, peak_of, jnp.zeros((padded, genes), jnp.float32))
    peak = jnp.max(best, axis=1, keepdims=True)
    scale = BINS / peak

    def weigh(index, carry):
        carry = list(carry)
        for block in range(nc):
            degree = degrees[index, block]
            position = jnp.clip(degree * scale - 0.5, 0.0, BINS - 1.0)
            for b in range(BINS):
                carry[b] = carry[b] + jnp.maximum(0.0, 1.0 - jnp.abs(position - b))
            carry[BINS] = carry[BINS] + degree
        return tuple(carry)

    totals = lax.fori_loop(0, nr, weigh, tuple(jnp.zeros((padded, genes), jnp.float32) for _ in range(BINS + 1)))
    lane = lax.broadcasted_iota(jnp.int32, (padded, 128), 1)
    line = lax.broadcasted_iota(jnp.int32, (padded, 128), 0)
    freq = jnp.zeros((padded, 128), jnp.float32)
    for b in range(BINS):
        freq = jnp.where(lane == b, jnp.sum(totals[b], axis=1, keepdims=True), freq)
    freq = freq / genes_all
    freq_ref[...] = freq[:npower, :BINS]
    mean_log = jnp.log(jnp.sum(totals[BINS], axis=1, keepdims=True) / genes_all) * LOG10E
    inside = lane < BINS
    xfit = jnp.log((lane.astype(jnp.float32) + 0.5) * peak / BINS) * LOG10E
    yfit = jnp.log(freq + 1.0 / genes_all) * LOG10E

    def deviation(values):
        mean = jnp.sum(jnp.where(inside, values, 0.0), axis=1, keepdims=True) / BINS
        return jnp.where(inside, values - mean, 0.0)

    xdev, ydev = deviation(xfit), deviation(yfit)
    slope = jnp.sum(xdev * ydev, axis=1, keepdims=True) / jnp.sum(xdev * xdev, axis=1, keepdims=True)
    on_line = jnp.logical_and(lane == line, line < npower)
    slope_ref[...] = jnp.sum(jnp.where(on_line, slope, 0.0), axis=0, keepdims=True)[:, :npower]
    mean_log_ref[...] = jnp.sum(jnp.where(on_line, mean_log, 0.0), axis=0, keepdims=True)[:, :npower]

    lax.fori_loop(1, nr, lambda d, _: (deg_copy(d).wait_send(), 0)[1], 0)


def solution(mesh):
    nr, nc = mesh.shape["row"], mesh.shape["col"]

    def on_device(expression, powers):
        genes, samples = expression.shape
        npower = powers.shape[0]
        padded = -(-npower // 8) * 8
        if padded == npower:
            padded += 8
        vmem = pl.BlockSpec(memory_space=pltpu.VMEM)
        dma = pltpu.SemaphoreType.DMA
        log_degree, freq, slope, mean_log = pl.pallas_call(
            functools.partial(kernel, nr, nc, npower),
            out_shape=(
                jax.ShapeDtypeStruct((npower, genes), jnp.float32),
                jax.ShapeDtypeStruct((npower, BINS), jnp.float32),
                jax.ShapeDtypeStruct((1, npower), jnp.float32),
                jax.ShapeDtypeStruct((1, npower), jnp.float32),
            ),
            in_specs=[pl.BlockSpec(memory_space=pltpu.SMEM), vmem],
            out_specs=(vmem,) * 4,
            scratch_shapes=[
                pltpu.VMEM((nc, genes, samples), jnp.bfloat16),
                pltpu.VMEM((nr, genes, samples), jnp.bfloat16),
                pltpu.VMEM((nr, genes, 128), jnp.float32),
                pltpu.VMEM((nr, genes, 128), jnp.float32),
                pltpu.VMEM((nc, nc, padded, genes), jnp.float32),
                pltpu.VMEM((nr, nc, padded, genes), jnp.float32),
                dma((nc, HALVES)),
                dma((nc, HALVES)),
                dma((nc, HALVES)),
                dma((nr // 2,)),
                dma((nr // 2,)),
                dma((nr,)),
                dma((nc, nc)),
                dma((nc, nc)),
                dma((nr,)),
                dma((nr,)),
            ],
            compiler_params=pltpu.CompilerParams(
                collective_id=0, has_side_effects=True, vmem_limit_bytes=48 * 1024 * 1024
            ),
        )(powers, expression)
        return log_degree, freq, slope.reshape(npower), mean_log.reshape(npower)

    return jax.shard_map(
        on_device,
        mesh=mesh,
        in_specs=(P(("row", "col"), None), P()),
        out_specs=(P(None, ("row", "col")), P(), P(), P()),
        check_vma=False,
    )
```

time: 202 us -> 43.5 us (0.22)
  blocking collectives: 79.4 us -> 0 us
  waiting for transfers between devices: 77.6 us -> 0 us
  Pallas kernels: 0 us -> 38.9 us
  matrix products: 17.6 us -> 0 us
  between operations: 13.8 us -> 0.65 us
  other arithmetic: 10.3 us -> 0 us
    all_gather x2 -> x0, waiting for transfers between devices: 56.9 us -> none  [the longest x1 30.9 us: on_device(): left_genes = lax.all_gather(expression, 'col', axis=0, tiled=True)]
    psum x1 -> x0, blocking collectives: 40.9 us -> none  [on_device(): lax.psum((jnp.sum(weights, axis=1), jnp.sum(degree, axis=1)), ('row', 'co...]
    pallas_call x0 -> x1, Pallas kernels: none -> 38.9 us  [on_device(): pl.pallas_call(functools.partial(kernel, nr, nc, npower), out_shape=(jax....]
    pmax x1 -> x0, blocking collectives: 38.4 us -> none  [on_device(): peak = lax.pmax(jnp.max(degree, axis=1), ('row', 'col'))]
    reduce_scatter x1 -> x0, waiting for transfers between devices: 19.3 us -> none  [on_device(): lax.psum_scatter(row_totals, 'col', scatter_dimension=1, tiled=True)]
    dot_general x2 -> x0, matrix products: 17.6 us -> none  [one_block(): lax.dot_general(row_block, right_genes, (((1,), (1,)), ((), ())), preferr...]
    reduce_sum x9 -> x0, other arithmetic: 7.25 us -> none  [the longest x2 3.52 us: gene_stats(): gene_mean = jnp.mean(values, axis=1)]
    unnamed x8, local copies, waits for them, and re-layouts: 0.73 us -> 3.82 us
  transfers between devices with their start and end apart: 3 -> 0, of which waited for: 3 -> 0; matrix products, arithmetic and copies ran while one was open for 2% -> 0% of each run, Pallas kernels for 0% -> 0%
where the time goes in v1:
time: 43.5 us; the launch traced here: 43.3 us
  Pallas kernels  38.9 us (89%)
  local copies, waits for them, and re-layouts  3.82 us (9%)
  between operations  0.65 us (1%)
    pallas_call x1, Pallas kernels, on_device(): pl.pallas_call(functools.partial(kernel, nr, nc, npower), out_shape=(jax....  38.9 us
    unnamed x8, local copies, waits for them, and re-layouts  3.82 us

profile of v1, /device:TPU:0, one launch (start us, length us, event | category | flops | bytes accessed | tf_op | source)
XLA Modules:
  0.0 43.3 jit_solution(12480145247127720693)
XLA Ops:
  0.6 0.0 copy-start
  0.6 0.9 %copy-done = bf16[128,1024]{1,0:T(8,128)(2,1)S(1)} copy-done((bf16[128,1024]{1,0:T(8,128)(2,1)S(1)}, bf16[128,1024]{1,0:T(8,128)(2,1)}, u32[]{:S(2)}) %copy-start) | copy-done | bytes 262168
  1.6 0.0 copy-start.1
  1.6 0.7 %copy-done.1 = s32[10]{0:T(128)S(1)} copy-done((s32[10]{0:T(128)S(1)}, s32[10]{0:T(128)}, u32[]{:S(2)}) %copy-start.1) | copy-done | bytes 64
  2.2 38.9 %shard_map.57 = (f32[10,128]{1,0:T(8,128)S(1)}, f32[10,10]{1,0:T(8,128)S(1)}, f32[1,10]{1,0:T(1,128)S(1)}, f32[1,10]{1,0:T(1,128)S(1)}) custom-call(s32[10]{0:T(128)S(1)} %copy-done.1, bf16[128,1024]{1,0:T(8,128)(2,1)S(1)} %copy-done), custom_call_target="tpu_custom_call" | custom-call | tf_op jit(solution)/shard_map/pallas_call | solution.py:345
  41.1 0.6 %copy.10 = f32[10,128]{1,0:T(8,128)} copy(f32[10,128]{1,0:T(8,128)S(1)} %get-tuple-element.16) | data formatting | bytes 10240
  41.7 0.6 %copy.11 = f32[10,10]{1,0:T(8,128)} copy(f32[10,10]{1,0:T(8,128)S(1)} %get-tuple-element.17) | data formatting | bytes 800
  42.3 0.5 %copy.12 = f32[10]{0:T(128)} copy(f32[10]{0:T(128)S(1)} %bitcast.3) | data formatting | bytes 80
  42.8 0.5 %copy.13 = f32[10]{0:T(128)} copy(f32[10]{0:T(128)S(1)} %bitcast.2) | data formatting | bytes 80
Async XLA Ops:
  0.6 1.0 %copy-start = (bf16[128,1024]{1,0:T(8,128)(2,1)S(1)}, bf16[128,1024]{1,0:T(8,128)(2,1)}, u32[]{:S(2)}) copy-start(bf16[128,1024]{1,0:T(8,128)(2,1)} %expr_ref.1) | copy-start | bytes 786436
  1.6 0.7 %copy-start.1 = (s32[10]{0:T(128)S(1)}, s32[10]{0:T(128)}, u32[]{:S(2)}) copy-start(s32[10]{0:T(128)} %powers_ref.1) | copy-start | bytes 124

commit v2 on v1

--- a/solution.py
+++ b/solution.py
@@ -15,11 +15,11 @@
 MESH = pl.DeviceIdType.MESH
 
 
-def xor(value, mask):
-    result, bit = value, 1
-    while bit <= mask:
-        if mask & bit:
-            result = result + bit - 2 * bit * ((value // bit) % 2)
+def xor(value, mask, size):
+    result, bit = 0, 1
+    while bit < size:
+        one, two = (value // bit) % 2, (mask // bit) % 2
+        result = result + bit * (one + two - 2 * one * two)
         bit *= 2
     return result
 
@@ -33,8 +33,8 @@
 
 
 def kernel(
-    nr, nc, npower, powers_ref, expr_ref, log_degree_ref, freq_ref, slope_ref, mean_log_ref,
-    left, right, right_mean, right_inv, partial, degrees,
+    nr, nc, npower, powers_hbm, expr_hbm, degrees, own_degree,
+    powers_ref, expr_ref, left, right, right_mean, right_inv, left_stats, sums_ref, partial, load_sem,
     up_send, down_send, line_recv, plane_send, relay_send, plane_recv, part_send, part_recv, deg_send, deg_recv,
 ):
     r, c = lax.axis_index("row"), lax.axis_index("col")
@@ -47,23 +47,41 @@
     genes_all = genes * nr * nc
 
     def chip_partner(k):
-        return (xor(chip, k) if nq & (nq - 1) == 0 else (chip + k) % nq) * 2 + core
+        return (xor(chip, k, nq) if nq & (nq - 1) == 0 else (chip + k) % nq) * 2 + core
 
     def chip_source(k):
-        return (xor(chip, k) if nq & (nq - 1) == 0 else (chip + nq - k) % nq) * 2 + core
+        return (xor(chip, k, nq) if nq & (nq - 1) == 0 else (chip + nq - k) % nq) * 2 + core
+
+    def nth_source(n):
+        source, other = chip_source(n // 2), n % 2
+        return source + other * (1 - 2 * core)
+
+    loads = (
+        pltpu.make_async_copy(expr_hbm, expr_ref, load_sem.at[0]),
+        pltpu.make_async_copy(powers_hbm, powers_ref, load_sem.at[1]),
+    )
+    for load in loads:
+        load.start()
 
     barrier = pltpu.get_barrier_semaphore()
 
-    def greet_col(d, _):
-        pl.semaphore_signal(barrier, inc=1, device_id=(r, (c + d) % nc), device_id_type=MESH)
-        return 0
-
-    def greet_row(d, _):
-        pl.semaphore_signal(barrier, inc=1, device_id=((r + d) % nr, c), device_id_type=MESH)
-        return 0
-
-    lax.fori_loop(1, nc, greet_col, 0)
-    lax.fori_loop(1, nr, greet_row, 0)
+    def greet(row, col):
+        pl.semaphore_signal(barrier, inc=1, device_id=(row, col), device_id_type=MESH)
+
+    greet(twin, c)
+    for k in range(1, nq):
+        greet(chip_partner(k), c)
+
+    @pl.when(c + 1 < nc)
+    def _():
+        greet(r, c + 1)
+
+    @pl.when(c >= 1)
+    def _():
+        greet(r, c - 1)
+
+    for load in loads:
+        load.wait()
 
     left[c] = expr_ref[...]
     right[r] = expr_ref[...]
@@ -74,8 +92,7 @@
         right_mean[index] = jnp.broadcast_to(mean, (genes, 128))
         right_inv[index] = jnp.broadcast_to(inv, (genes, 128))
 
-    right_stats(r)
-    pl.semaphore_wait(barrier, nc - 1 + nr - 1)
+    pl.semaphore_wait(barrier, nq + jnp.minimum(1, nc - 1 - c) + jnp.minimum(1, c))
 
     def line_copy(step, half, up):
         block = (c - step) if up else (c + step)
@@ -142,13 +159,19 @@
             device_id=(r, (c + d) % nc), device_id_type=MESH,
         )
 
-    def run_pass(block):
+    def start_left(block):
+        mean, inv = gene_stats(left[block])
+        left_stats[block, 0] = jnp.broadcast_to(mean, (genes, 128)).T[0:8, :]
+        left_stats[block, 1] = jnp.broadcast_to(inv, (genes, 128)).T[0:8, :]
+
+    def run_part(block, first, last):
+        if first == last:
+            return
         genes_left = left[block]
-        mean, inv = gene_stats(genes_left)
-        mean_row = jnp.broadcast_to(mean, (genes, 128)).T[0:1, :]
-        inv_row = jnp.broadcast_to(inv, (genes, 128)).T[0:1, :]
-
-        def one_right(index, sums):
+        mean_row, inv_row = left_stats[block, 0, 0:1, :], left_stats[block, 1, 0:1, :]
+
+        def one_right(turn, sums):
+            index = nth_source(turn)
             raw = lax.dot_general(
                 right[index], genes_left, (((1,), (1,)), ((), ())), preferred_element_type=jnp.float32
             )
@@ -159,9 +182,14 @@
                 for p in range(npower)
             )
 
-        sums = lax.fori_loop(
-            0, nr, one_right, tuple(jnp.zeros((8, genes), jnp.float32) for _ in range(npower)), unroll=2
-        )
+        start = tuple(
+            sums_ref[block, p] if first else jnp.zeros((8, genes), jnp.float32) for p in range(npower)
+        )
+        sums = lax.fori_loop(first, last, one_right, start, unroll=2)
+        if last < nr:
+            for p in range(npower):
+                sums_ref[block, p] = sums[p]
+            return
         lines = [jnp.sum(total, axis=0, keepdims=True) for total in sums]
         lines.append(jnp.zeros((padded - npower, genes), jnp.float32))
         partial[c, block] = jnp.concatenate(lines, axis=0)
@@ -171,6 +199,18 @@
             return 0
 
         lax.fori_loop(1, nc, send, 0)
+
+    def both_ways(step, work):
+        def one(way, _):
+            block = c + step * (2 * way - 1)
+
+            @pl.when(jnp.logical_and(block >= 0, block < nc))
+            def _():
+                work(block)
+
+            return 0
+
+        lax.fori_loop(0, 2, one, 0)
 
     def line_step(step, half):
         for up in (True, False):
@@ -183,44 +223,54 @@
                 def _():
                     line_copy(step, half, up).start()
 
-    def plane_step(k):
-        if k:
-            source = chip_source(k)
+    def plane_steps(ks):
+        for k in ks:
+            plane_arrival(chip_source(k)).wait_recv()
+            relay_copy(k).start()
+            right_stats(chip_source(k))
+
+    def twin_steps(ks):
+        for k in ks:
+            source = nth_source(2 * k + 1)
             plane_arrival(source).wait_recv()
-            relay_copy(k).start()
             right_stats(source)
 
-    def twin_step(k):
-        source = chip_source(k) + 1 - 2 * core
-        plane_arrival(source).wait_recv()
-        right_stats(source)
-
-    def passes(step):
-        for up in (True, False):
-            @pl.when(c - step >= 0 if up else c + step < nc)
-            def _():
-                run_pass(jnp.clip(c - step if up else c + step, 0, nc - 1))
-
-    twin_step(0)
-    todo = list(range(1, nq))
-    for step in range(1, nc):
-        last_plane = step == 2 or nc == 2
-        for half in range(HALVES):
-            line_step(step, half)
-        if step == 1:
-            for k in todo[: max(1, nq - 2)]:
-                plane_step(k)
-            for k in todo[: max(1, nq - 2)]:
-                twin_step(k)
-        if last_plane:
-            for k in todo[max(1, nq - 2):]:
-                plane_step(k)
-            for k in todo[max(1, nq - 2):]:
-                twin_step(k)
-            run_pass(c)
-            passes(1)
-        if step >= 2:
-            passes(step)
+    near = list(range(1, max(1, nq - 1)))
+    far = list(range(max(1, nq - 1), nq))
+    some = 2 * (1 + len(near))
+    if some == nr:
+        some = 2
+
+    right_stats(r)
+    start_left(c)
+    twin_steps([0])
+    run_part(c, 0, 2)
+    for half in range(HALVES):
+        line_step(1, half)
+    plane_steps(near)
+    both_ways(1, start_left)
+    twin_steps(near)
+    run_part(c, 2, some)
+    if nc > 2:
+        line_step(2, 0)
+    both_ways(1, lambda block: run_part(block, 0, some))
+    if nc > 2:
+        for half in range(1, HALVES):
+            line_step(2, half)
+    plane_steps(far)
+    twin_steps(far)
+    run_part(c, some, nr)
+    both_ways(1, lambda block: run_part(block, some, nr))
+
+    def whole(block):
+        start_left(block)
+        run_part(block, 0, nr)
+
+    for step in range(2, nc):
+        if step > 2:
+            for half in range(HALVES):
+                line_step(step, half)
+        both_ways(step, whole)
 
     def part_wait(d, _):
         source = (c + d) % nc
@@ -236,11 +286,16 @@
         return lax.fori_loop(0, nc, one, 0)
 
     lax.fori_loop(1, nc, part_wait, 0)
+    lines = []
     for block in range(nc):
         total = partial[0, block]
         for source in range(1, nc):
             total = total + partial[source, block]
-        degrees[r, block] = total
+        lines.append(total[:npower])
+    spare = degrees.shape[1] - nc * npower
+    if spare:
+        lines.append(jnp.zeros((spare, genes), jnp.float32))
+    degrees[r] = jnp.concatenate(lines, axis=0)
 
     def deg_copy(d):
         return pltpu.make_async_remote_copy(
@@ -263,7 +318,10 @@
         return 0
 
     lax.fori_loop(1, nr, deg_start, 0)
-    log_degree_ref[...] = (jnp.log(degrees[r, c]) * LOG10E)[:npower]
+    own = partial[0, c]
+    for source in range(1, nc):
+        own = own + partial[source, c]
+    own_degree[...] = own
 
     for half in range(HALVES):
         for up in (True, False):
@@ -286,34 +344,48 @@
     lax.fori_loop(1, nc, part_done, 0)
     lax.fori_loop(1, nr, deg_wait, 0)
 
-    def peak_of(index, best):
-        for block in range(nc):
-            best = jnp.maximum(best, degrees[index, block])
-        return best
-
-    best = lax.fori_loop(0, nr, peak_of, jnp.zeros((padded, genes), jnp.float32))
-    peak = jnp.max(best, axis=1, keepdims=True)
-    scale = BINS / peak
+    lax.fori_loop(1, nr, lambda d, _: (deg_copy(d).wait_send(), 0)[1], 0)
+
+
+def fit_kernel(nr, nc, npower, degrees, own_degree, log_degree_ref, freq_ref, slope_ref, mean_log_ref):
+    height, genes = degrees.shape[1:]
+    padded = own_degree.shape[0]
+    genes_all = genes * nr * nc
+    spare = height - nc * npower
+    log_degree_ref[...] = (jnp.log(own_degree[...]) * LOG10E)[:npower]
+
+    def fold(values, combine):
+        total = values[:npower]
+        for block in range(1, nc):
+            total = combine(total, values[block * npower:(block + 1) * npower])
+        return jnp.concatenate([total, jnp.ones((padded - npower, 1), jnp.float32)], axis=0)
+
+    best = lax.fori_loop(1, nr, lambda index, best: jnp.maximum(best, degrees[index]), degrees[0])
+    peak = fold(jnp.max(best, axis=1, keepdims=True), jnp.maximum)
+    scales = [(BINS / peak)[:npower]] * nc
+    if spare:
+        scales.append(jnp.ones((spare, 1), jnp.float32))
+    scale = jnp.broadcast_to(jnp.concatenate(scales, axis=0), (height, genes))
 
     def weigh(index, carry):
         carry = list(carry)
-        for block in range(nc):
-            degree = degrees[index, block]
-            position = jnp.clip(degree * scale - 0.5, 0.0, BINS - 1.0)
-            for b in range(BINS):
-                carry[b] = carry[b] + jnp.maximum(0.0, 1.0 - jnp.abs(position - b))
-            carry[BINS] = carry[BINS] + degree
+        degree = degrees[index]
+        position = jnp.clip(degree * scale - 0.5, 0.0, BINS - 1.0)
+        for b in range(BINS):
+            carry[b] = carry[b] + jnp.maximum(0.0, 1.0 - jnp.abs(position - b))
+        carry[BINS] = carry[BINS] + degree
         return tuple(carry)
 
-    totals = lax.fori_loop(0, nr, weigh, tuple(jnp.zeros((padded, genes), jnp.float32) for _ in range(BINS + 1)))
+    totals = lax.fori_loop(0, nr, weigh, tuple(jnp.zeros((height, genes), jnp.float32) for _ in range(BINS + 1)))
+    totals = [fold(jnp.sum(total, axis=1, keepdims=True), jnp.add) for total in totals]
     lane = lax.broadcasted_iota(jnp.int32, (padded, 128), 1)
     line = lax.broadcasted_iota(jnp.int32, (padded, 128), 0)
     freq = jnp.zeros((padded, 128), jnp.float32)
     for b in range(BINS):
-        freq = jnp.where(lane == b, jnp.sum(totals[b], axis=1, keepdims=True), freq)
+        freq = jnp.where(lane == b, totals[b], freq)
     freq = freq / genes_all
     freq_ref[...] = freq[:npower, :BINS]
-    mean_log = jnp.log(jnp.sum(totals[BINS], axis=1, keepdims=True) / genes_all) * LOG10E
+    mean_log = jnp.log(totals[BINS] / genes_all) * LOG10E
     inside = lane < BINS
     xfit = jnp.log((lane.astype(jnp.float32) + 0.5) * peak / BINS) * LOG10E
     yfit = jnp.log(freq + 1.0 / genes_all) * LOG10E
@@ -327,8 +399,6 @@
     on_line = jnp.logical_and(lane == line, line < npower)
     slope_ref[...] = jnp.sum(jnp.where(on_line, slope, 0.0), axis=0, keepdims=True)[:, :npower]
     mean_log_ref[...] = jnp.sum(jnp.where(on_line, mean_log, 0.0), axis=0, keepdims=True)[:, :npower]
-
-    lax.fori_loop(1, nr, lambda d, _: (deg_copy(d).wait_send(), 0)[1], 0)
 
 
 def solution(mesh):
@@ -340,25 +410,29 @@
         padded = -(-npower // 8) * 8
         if padded == npower:
             padded += 8
+        height = -(-npower * nc // 8) * 8
         vmem = pl.BlockSpec(memory_space=pltpu.VMEM)
+        hbm = pl.BlockSpec(memory_space=pltpu.HBM)
         dma = pltpu.SemaphoreType.DMA
-        log_degree, freq, slope, mean_log = pl.pallas_call(
+        degrees, own_degree = pl.pallas_call(
             functools.partial(kernel, nr, nc, npower),
             out_shape=(
-                jax.ShapeDtypeStruct((npower, genes), jnp.float32),
-                jax.ShapeDtypeStruct((npower, BINS), jnp.float32),
-                jax.ShapeDtypeStruct((1, npower), jnp.float32),
-                jax.ShapeDtypeStruct((1, npower), jnp.float32),
+                jax.ShapeDtypeStruct((nr, height, genes), jnp.float32),
+                jax.ShapeDtypeStruct((padded, genes), jnp.float32),
             ),
-            in_specs=[pl.BlockSpec(memory_space=pltpu.SMEM), vmem],
-            out_specs=(vmem,) * 4,
+            in_specs=[hbm, hbm],
+            out_specs=(vmem, vmem),
             scratch_shapes=[
+                pltpu.SMEM((npower,), jnp.int32),
+                pltpu.VMEM((genes, samples), jnp.bfloat16),
                 pltpu.VMEM((nc, genes, samples), jnp.bfloat16),
                 pltpu.VMEM((nr, genes, samples), jnp.bfloat16),
                 pltpu.VMEM((nr, genes, 128), jnp.float32),
                 pltpu.VMEM((nr, genes, 128), jnp.float32),
+                pltpu.VMEM((nc, 2, 8, genes), jnp.float32),
+                pltpu.VMEM((nc, npower, 8, genes), jnp.float32),
                 pltpu.VMEM((nc, nc, padded, genes), jnp.float32),
-                pltpu.VMEM((nr, nc, padded, genes), jnp.float32),
+                dma((2,)),
                 dma((nc, HALVES)),
                 dma((nc, HALVES)),
                 dma((nc, HALVES)),
@@ -371,9 +445,20 @@
                 dma((nr,)),
             ],
             compiler_params=pltpu.CompilerParams(
-                collective_id=0, has_side_effects=True, vmem_limit_bytes=48 * 1024 * 1024
+                collective_id=0, has_side_effects=True, vmem_limit_bytes=67043328
             ),
         )(powers, expression)
+        log_degree, freq, slope, mean_log = pl.pallas_call(
+            functools.partial(fit_kernel, nr, nc, npower),
+            out_shape=(
+                jax.ShapeDtypeStruct((npower, genes), jnp.float32),
+                jax.ShapeDtypeStruct((npower, BINS), jnp.float32),
+                jax.ShapeDtypeStruct((1, npower), jnp.float32),
+                jax.ShapeDtypeStruct((1, npower), jnp.float32),
+            ),
+            in_specs=[vmem, vmem],
+            out_specs=(vmem,) * 4,
+        )(degrees, own_degree)
         return log_degree, freq, slope.reshape(npower), mean_log.reshape(npower)
 
     return jax.shard_map(

time: 43.5 us -> 38.7 us (0.89)
  local copies, waits for them, and re-layouts: 3.82 us -> 0 us
  Pallas kernels: 38.9 us -> 37.9 us
    unnamed x8 -> x0, local copies, waits for them, and re-layouts: 3.82 us -> none
    pallas_call x1, Pallas kernels: 38.9 us -> 35.4 us  [on_device(): pl.pallas_call(functools.partial(kernel, nr, nc, npower), out_shape=(jax....]
    pallas_call x0 -> x1, Pallas kernels: none -> 2.44 us  [on_device(): pl.pallas_call(functools.partial(fit_kernel, nr, nc, npower), out_shape=(...]
where the time goes in v2:
time: 38.7 us; the launch traced here: 38.5 us
  Pallas kernels  37.9 us (98%)
  between operations  0.64 us (2%)
    pallas_call x1, Pallas kernels, on_device(): pl.pallas_call(functools.partial(kernel, nr, nc, npower), out_shape=(jax....  35.4 us
    pallas_call x1, Pallas kernels, on_device(): pl.pallas_call(functools.partial(fit_kernel, nr, nc, npower), out_shape=(...  2.44 us

profile of v2, /device:TPU:0, one launch (start us, length us, event | category | flops | bytes accessed | tf_op | source)
XLA Modules:
  0.0 38.5 jit_solution(4965054083452780049)
XLA Ops:
  0.6 35.4 %shard_map.57 = (f32[8,40,128]{2,1,0:T(8,128)}, f32[16,128]{1,0:T(8,128)}) custom-call(s32[10]{0:T(128)} %powers_hbm.1, bf16[128,1024]{1,0:T(8,128)(2,1)} %expr_hbm.1), custom_call_target="tpu_custom_call" | custom-call | tf_op jit(solution)/shard_map/pallas_call | solution.py:417
  36.1 2.4 %shard_map.58 = (f32[10,128]{1,0:T(8,128)}, f32[10,10]{1,0:T(8,128)}, f32[1,10]{1,0:T(1,128)}, f32[1,10]{1,0:T(1,128)}) custom-call(f32[8,40,128]{2,1,0:T(8,128)} %get-tuple-element.10.degrees, f32[16,128]{1,0:T(8,128)} %get-tuple-element.11.own_degree), custom_call_target="tpu_custom_call" | custom-call | tf_op jit(solution)/shard_map/pallas_call | solution.py:451

commit v3 on v2

--- a/solution.py
+++ b/solution.py
@@ -249,15 +249,15 @@
         line_step(1, half)
     plane_steps(near)
     both_ways(1, start_left)
+    if nc > 2:
+        line_step(2, 0)
     twin_steps(near)
     run_part(c, 2, some)
-    if nc > 2:
-        line_step(2, 0)
-    both_ways(1, lambda block: run_part(block, 0, some))
     if nc > 2:
         for half in range(1, HALVES):
             line_step(2, half)
     plane_steps(far)
+    both_ways(1, lambda block: run_part(block, 0, some))
     twin_steps(far)
     run_part(c, some, nr)
     both_ways(1, lambda block: run_part(block, some, nr))

time: 38.7 us -> 37.8 us (0.977)
  Pallas kernels: 37.9 us -> 37.1 us
    pallas_call x1, Pallas kernels: 35.4 us -> 34.6 us  [on_device(): pl.pallas_call(functools.partial(kernel, nr, nc, npower), out_shape=(jax....]
where the time goes in v3:
time: 37.8 us; the launch traced here: 37.7 us
  Pallas kernels  37.1 us (98%)
  between operations  0.64 us (2%)
    pallas_call x1, Pallas kernels, on_device(): pl.pallas_call(functools.partial(kernel, nr, nc, npower), out_shape=(jax....  34.6 us
    pallas_call x1, Pallas kernels, on_device(): pl.pallas_call(functools.partial(fit_kernel, nr, nc, npower), out_shape=(...  2.44 us

profile of v3, /device:TPU:0, one launch (start us, length us, event | category | flops | bytes accessed | tf_op | source)
XLA Modules:
  0.0 37.7 jit_solution(3829636109478419388)
XLA Ops:
  0.6 34.6 %shard_map.57 = (f32[8,40,128]{2,1,0:T(8,128)}, f32[16,128]{1,0:T(8,128)}) custom-call(s32[10]{0:T(128)} %powers_hbm.1, bf16[128,1024]{1,0:T(8,128)(2,1)} %expr_hbm.1), custom_call_target="tpu_custom_call" | custom-call | tf_op jit(solution)/shard_map/pallas_call | solution.py:417
  35.3 2.4 %shard_map.58 = (f32[10,128]{1,0:T(8,128)}, f32[10,10]{1,0:T(8,128)}, f32[1,10]{1,0:T(1,128)}, f32[1,10]{1,0:T(1,128)}) custom-call(f32[8,40,128]{2,1,0:T(8,128)} %get-tuple-element.10.degrees, f32[16,128]{1,0:T(8,128)} %get-tuple-element.11.own_degree), custom_call_target="tpu_custom_call" | custom-call | tf_op jit(solution)/shard_map/pallas_call | solution.py:451
